TPU v7x, 32 devices: a whole 2x2x4 slice. The times are simulated.
32 devices in a mesh: heads: 4 (over y, core), blk: 8 (over z, x).
Axes of the slice: x: 2, y: 2, z: 4, core: 2. Of those that a mesh axis runs over, the one named last changes fastest.
Arguments:
- tokens: bfloat16 [4096, 4096], P(('blk', 'heads')), may hold values from -6 to 6
- w_query: bfloat16 [4096, 2048], P('blk', 'heads'), may hold values from -0.75 to 0.75
- key_value_weight: bfloat16 [4096, 2, 512], P('blk', None, 'heads'), may hold values from -0.75 to 0.75
- w_out: bfloat16 [2048, 4096], P(('heads', 'blk')), may hold values from -0.5 to 0.5
- doc_lengths: int32 [16], replicated, may hold values from 1 to 1024, 4096 in all
Outputs:
- attended: bfloat16 [4096, 4096], P(('blk', 'heads'))
Inputs may be any that keep to these rules, and one draw needn't show every extreme that they name: `doc_lengths`: the 16 lengths sum to 4096; the longest document has exactly 1024 tokens.
All inputs are finite; a program needn't handle non-finite values.
Results may differ from a plain program's by a relative error of at most 0.012.
Values may be sent and summed in bfloat16 or wider, within the bound.
A program may use at most 128 MiB of HBM per device.

v0:
```python
import jax
import jax.numpy as jnp
from jax import lax
from jax.sharding import PartitionSpec as P

HEAD_SIZE = 128
norm_epsilon = 1e-05
rope_base = 500000.0
masked_score = -1e30


def shifted(value, axis, steps):
    count = lax.axis_size(axis)
    first, last = (max(0, -steps), min(count, count - steps))
    return lax.ppermute(value, axis, [(source, source + steps) for source in range(first, last)])


def locate_documents(positions, doc_lengths):
    ends = jnp.cumsum(doc_lengths)
    after = positions[:, None] >= ends[None, :]
    ident = jnp.sum(after.astype(jnp.int32), axis=1)
    starts = jnp.sum(jnp.where(after, doc_lengths[None, :], 0), axis=1)
    return (ident, starts)


def apply_rotation(values, relative_offset):
    half = values.shape[-1] // 2
    freqs = jnp.power(rope_base, -2.0 * jnp.arange(half, dtype=jnp.float32) / values.shape[-1])
    angle = relative_offset.astype(jnp.float32)[:, None] * freqs[None, :]
    cosine = jnp.cos(angle)[:, None, :]
    sine = jnp.sin(angle)[:, None, :]
    first = values[..., :half]
    second = values[..., half:]
    return jnp.concatenate(
        [first * cosine - second * sine, second * cosine + first * sine], axis=-1
    )


def on_device(tokens, w_query, key_value_weight, w_out, doc_lengths):
    blk_index = lax.axis_index("blk")
    reach = lax.axis_size("blk") // 4
    values = tokens.astype(jnp.float32)
    normalized_input = (
        values * lax.rsqrt(jnp.mean(values * values, axis=1, keepdims=True) + norm_epsilon)
    ).astype(jnp.bfloat16)
    block_input = lax.all_gather(normalized_input, "heads", axis=0, tiled=True)
    block_rows = block_input.shape[0]
    query_cols = w_query.shape[1]
    kv_cols = key_value_weight.shape[2]
    pieces = (
        lax.all_gather(w_query, "blk", axis=0, tiled=True),
        lax.all_gather(key_value_weight, "blk", axis=0, tiled=True),
    )
    count = pieces[0].shape[0]
    query_part = jnp.dot(block_input, pieces[0], preferred_element_type=jnp.float32)
    keyval_part = jnp.dot(
        block_input, pieces[1].reshape(count, 2 * kv_cols), preferred_element_type=jnp.float32
    )
    positions = blk_index * block_rows + jnp.arange(block_rows, dtype=jnp.int32)
    ident, starts = locate_documents(positions, doc_lengths)
    relative_offset = positions - starts
    query_heads = query_cols // HEAD_SIZE
    kv_heads = kv_cols // HEAD_SIZE
    head_group = query_heads // kv_heads
    query_rows = apply_rotation(
        query_part.reshape(block_rows, query_heads, HEAD_SIZE), relative_offset
    ).astype(jnp.bfloat16)
    query_rows = query_rows.reshape(block_rows, kv_heads, head_group, HEAD_SIZE)
    rotated_keys = apply_rotation(
        keyval_part[:, :kv_cols].reshape(block_rows, kv_heads, HEAD_SIZE), relative_offset
    ).astype(jnp.bfloat16)
    value_rows = (
        keyval_part[:, kv_cols:].reshape(block_rows, kv_heads, HEAD_SIZE).astype(jnp.bfloat16)
    )
    kv_block = jnp.stack([rotated_keys, value_rows], axis=1)
    scale = HEAD_SIZE ** (-0.5)

    def attend_tile(state, kv_now, distance):
        key_pos = (blk_index - distance) * block_rows + jnp.arange(block_rows, dtype=jnp.int32)
        key_doc, unused_k = locate_documents(key_pos, doc_lengths)
        keep = (
            (key_pos[None, :] >= 0)
            & (key_pos[None, :] <= positions[:, None])
            & (key_doc[None, :] == ident[:, None])
        )
        highest, totals, accum = state
        scores = (
            jnp.einsum(
                "qhgd,khd->hgqk", query_rows, kv_now[:, 0], preferred_element_type=jnp.float32
            )
            * scale
        )
        scores = jnp.where(keep, scores, masked_score)
        new_high = jnp.maximum(highest, jnp.max(scores, axis=-1))
        fading = jnp.exp(highest - new_high)
        probs = jnp.where(keep, jnp.exp(scores - new_high[..., None]), 0.0)
        totals = totals * fading + jnp.sum(probs, axis=-1)
        update = jnp.einsum(
            "hgqk,khd->hgqd",
            probs.astype(jnp.bfloat16),
            kv_now[:, 1],
            preferred_element_type=jnp.float32,
        )
        accum = accum * fading[..., None] + update
        return (new_high, totals, accum)

    initial = (
        jnp.full((kv_heads, head_group, block_rows), masked_score, jnp.float32),
        jnp.zeros((kv_heads, head_group, block_rows), jnp.float32),
        jnp.zeros((kv_heads, head_group, block_rows, HEAD_SIZE), jnp.float32),
    )
    state = attend_tile(initial, kv_block, 0)

    def advance(distance, carry):
        kv_now, inner = carry
        kv_now = shifted(kv_now, "blk", 1)
        return (kv_now, attend_tile(inner, kv_now, distance))

    unused_kv, state = lax.fori_loop(1, reach + 1, advance, (kv_block, state))
    highest, totals, accum = state
    mixed = accum / totals[..., None]
    mixed = mixed.transpose(2, 0, 1, 3).reshape(block_rows, query_cols).astype(jnp.bfloat16)
    head_rows = lax.all_gather(w_out, "blk", axis=0, tiled=True)
    return lax.psum_scatter(
        jnp.dot(mixed, head_rows, preferred_element_type=jnp.float32).astype(jnp.bfloat16),
        "heads",
        scatter_dimension=0,
        tiled=True,
    )


def solution(mesh):
    return jax.shard_map(
        on_device,
        mesh=mesh,
        in_specs=(
            P(("blk", "heads"), None),
            P("blk", "heads"),
            P("blk", None, "heads"),
            P(("heads", "blk"), None),
            P(),
        ),
        out_specs=P(("blk", "heads"), None),
        check_vma=False,
    )
```

profile of v0, /device:TPU:0, one launch (start us, length us, event | category | flops | bytes accessed | tf_op | source)
XLA Modules:
  0.0 311.8 jit_solution(1493680241664175790)
XLA Ops:
  6.5 0.7 all-gather.7.cloned.1.call-update
  7.3 1.5 fusion.24
  8.8 2.5 fusion.25
  11.4 0.7 all-gather.9.cloned.1.call-update
  12.1 0.5 all-gather.11.cloned.1.call-update
  13.0 1.0 multiply_cosine_fusion
  14.0 0.4 compare_and_fusion.1
  14.4 46.9 %all-gather.7.cloned.1.call-done = bf16[4096,2,128]{2,1,0:T(2,128)(2,1)} async-done(((bf16[512,2,128]{2,1,0:T(2,128)(2,1)}), bf16[4096,2,128]{2,1,0:T(2,128)(2,1)}) %all-gather.7.cloned.1.call-update) | async-done | bytes 2097168 | tf_op jit(solution)/shard_map/all_gather | solution.py:52
  61.3 34.6 %all-gather.5.cloned.1.call-done = bf16[512,4096]{1,0:T(8,128)(2,1)} async-done(((bf16[128,4096]{1,0:T(8,128)(2,1)}), bf16[512,4096]{1,0:T(8,128)(2,1)}) %all-gather.5.cloned.1.call-update) | async-done | bytes 4194320 | tf_op jit(solution)/shard_map/all_gather | solution.py:46
  95.9 4.2 %fusion.27 = f32[512,256]{0,1:T(8,128)S(1)} fusion(bf16[512,4096]{1,0:T(8,128)(2,1)} %all-gather.5.cloned.1.call-done, bf16[512,8,2,128]{3,2,1,0:T(2,128)(2,1)} %bitcast.161), kind=kOutput, calls=%fused_computation.38 | convolution fusion | flops 1073741824 | bytes 6815744 | tf_op jit(solution)/shard_map/dot_general | solution.py:56
  100.1 0.6 fusion.48
  100.9 0.8 copy.35
  101.7 69.1 %all-gather.9.cloned.1.call-done = bf16[4096,512]{1,0:T(8,128)(2,1)} async-done(((bf16[512,512]{1,0:T(8,128)(2,1)}), bf16[4096,512]{1,0:T(8,128)(2,1)}) %all-gather.9.cloned.1.call-update) | async-done | bytes 4194320 | tf_op jit(solution)/shard_map/all_gather | solution.py:51
  170.8 5.8 %fusion.64 = f32[512,512]{0,1:T(8,128)S(1)} fusion(bf16[512,4096]{1,0:T(8,128)(2,1)} %all-gather.5.cloned.1.call-done, bf16[4096,512]{1,0:T(8,128)(2,1)} %all-gather.9.cloned.1.call-done), kind=kOutput, calls=%fused_computation.92 | convolution fusion | flops 2147483648 | bytes 9437184 | tf_op jit(solution)/shard_map/dot_general | solution.py:55
  178.1 1.2 fusion.21
  179.3 1.0 fusion.23
  180.4 1.6 fusion.36
  182.0 29.8 %while.22 = (s32[]{:T(128)}, bf16[512,2,1,128]{3,0,2,1:T(8,128)(2,1)S(1)}, f32[1,4,512]{2,1,0:T(4,128)S(1)}, f32[1,4,512]{2,1,0:T(4,128)S(1)}, f32[1,4,512,128]{...) while((s32[]{:T(128)}, ...), condition=%wide.region_10.11_spmd.clone, body=%wide.region_6.10_spmd.clone.sunk | while | flops 552107520 | bytes 18236672 | solution.py:119
  182.2 2.5 collective-permute-start
  185.1 6.1 %collective-permute-done = bf16[512,2,1,128]{3,0,2,1:T(8,128)(2,1)S(1)} collective-permute-done((bf16[512,2,1,128]{3,0,2,1:T(8,128)(2,1)S(1)}, bf16[512,2,1,128]{3,0,2,1:T(8,128)(2,1)S(1)}, u32[]{:S(2)}, u32[]{:S(2)}) %collective-permute-start) | collective-permute-done | bytes 262176 | tf_op jit(solution)/shard_map/while/body/eval_jaxpr/ppermute | solution.py:15
  191.2 0.9 fusion.76
  192.1 1.0 fusion.78
  193.2 1.9 fusion.79
  195.2 8.8 %collective-permute-start = (bf16[512,2,1,128]{3,0,2,1:T(8,128)(2,1)S(1)}, bf16[512,2,1,128]{3,0,2,1:T(8,128)(2,1)S(1)}, u32[]{:S(2)}, u32[]{:S(2)}) collective-permute-start(bf16[512,2,1,128]{3,0,2,1:T(8,128)(2,1)S(1)} %get-tuple-element.431), channel_id=1, source_target_pairs={{0,1},{1,2},{2,3},{3,4},{4,5},{5,6},{6,7},{8,9},{9,10},{10,11},{11... | collective-permute-start | bytes 786440 | tf_op jit(solution)/shard_map/while/body/eval_jaxpr/ppermute | solution.py:15
  204.1 0.3 compare_and_fusion.3
  204.4 3.4 %collective-permute-done = bf16[512,2,1,128]{3,0,2,1:T(8,128)(2,1)S(1)} collective-permute-done((bf16[512,2,1,128]{3,0,2,1:T(8,128)(2,1)S(1)}, bf16[512,2,1,128]{3,0,2,1:T(8,128)(2,1)S(1)}, u32[]{:S(2)}, u32[]{:S(2)}) %collective-permute-start) | collective-permute-done | bytes 262176 | tf_op jit(solution)/shard_map/while/body/eval_jaxpr/ppermute | solution.py:15
  207.8 0.9 fusion.76
  208.7 1.0 fusion.78
  209.8 1.9 fusion.79
  212.2 41.3 %all-gather.11.cloned.1.call-done = bf16[512,4096]{1,0:T(8,128)(2,1)} async-done(((bf16[64,4096]{1,0:T(8,128)(2,1)}), bf16[512,4096]{1,0:T(8,128)(2,1)}) %all-gather.11.cloned.1.call-update) | async-done | bytes 4194320 | tf_op jit(solution)/shard_map/all_gather | solution.py:123
  253.6 6.5 %convolution_convert_fusion = bf16[512,4096]{1,0:T(8,128)(2,1)} fusion(bf16[512,512]{0,1:T(8,128)(2,1)S(1)} %bitcast.151, bf16[512,4096]{1,0:T(8,128)(2,1)} %all-gather.11.cloned.1.call-done), kind=kOutput, calls=%fused_computation.27 | convolution fusion | flops 2149580800 | bytes 8912896 | tf_op jit(solution)/shard_map/dot_general | solution.py:125
  260.1 45.2 %reduce-scatter.2.cloned.1.call-done = bf16[128,4096]{1,0:T(8,128)(2,1)} async-done(((bf16[512,4096]{1,0:T(8,128)(2,1)}), bf16[128,4096]{1,0:T(8,128)(2,1)}) %reduce-scatter.2.cloned.1.call-update) | async-done | bytes 1048592 | tf_op jit(solution)/shard_map/reduce_scatter | solution.py:124
  (49 shorter events, 3.2 us)
Async XLA Ops:
  6.5 6.2 %copy-start.3 = (s32[16]{0:T(128)S(1)}, s32[16]{0:T(128)}, u32[]{:S(2)}) copy-start(s32[16]{0:T(128)} %param.11) | copy-start | bytes 196
  6.5 54.8 %all-gather.7.cloned.1.call-start = ((), (), s32[]{:S(2)}) async-start(), calls=%async_computation.2 | async-start | bytes 2359296 | tf_op jit(solution)/shard_map/all_gather | solution.py:52
  7.3 88.6 %all-gather.5.cloned.1.call-start = ((), (), s32[]{:S(2)}) async-start(), calls=%async_computation.1 | async-start | bytes 5242880 | tf_op jit(solution)/shard_map/all_gather | solution.py:46
  11.3 159.5 %all-gather.9.cloned.1.call-start = ((), (), s32[]{:S(2)}) async-start(), calls=%async_computation.3 | async-start | bytes 4718592 | tf_op jit(solution)/shard_map/all_gather | solution.py:51
  12.1 241.5 %all-gather.11.cloned.1.call-start = ((), (), s32[]{:S(2)}) async-start(), calls=%async_computation.4 | async-start | bytes 4718592 | tf_op jit(solution)/shard_map/all_gather | solution.py:123
  12.6 292.7 %reduce-scatter.2.cloned.1.call-start = ((), (), s32[]{:S(2)}) async-start(), calls=%async_computation.5 | async-start | bytes 5242880 | tf_op jit(solution)/shard_map/reduce_scatter | solution.py:124
  100.0 0.8 copy-start
  178.1 2.3 copy-start.1
  180.4 1.6 copy-start.2
  182.2 9.1 %collective-permute-start = (bf16[512,2,1,128]{3,0,2,1:T(8,128)(2,1)S(1)}, bf16[512,2,1,128]{3,0,2,1:T(8,128)(2,1)S(1)}, u32[]{:S(2)}, u32[]{:S(2)}) collective-permute-start(bf16[512,2,1,128]{3,0,2,1:T(8,128)(2,1)S(1)} %get-tuple-element.431), channel_id=1, source_target_pairs={{0,1},{1,2},{2,3},{3,4},{4,5},{5,6},{6,7},{8,9},{9,10},{10,11},{11... | collective-permute-start | bytes 786440 | tf_op jit(solution)/shard_map/while/body/eval_jaxpr/ppermute | solution.py:15
  195.2 12.7 %collective-permute-start = (bf16[512,2,1,128]{3,0,2,1:T(8,128)(2,1)S(1)}, bf16[512,2,1,128]{3,0,2,1:T(8,128)(2,1)S(1)}, u32[]{:S(2)}, u32[]{:S(2)}) collective-permute-start(bf16[512,2,1,128]{3,0,2,1:T(8,128)(2,1)S(1)} %get-tuple-element.431), channel_id=1, source_target_pairs={{0,1},{1,2},{2,3},{3,4},{4,5},{5,6},{6,7},{8,9},{9,10},{10,11},{11... | collective-permute-start | bytes 786440 | tf_op jit(solution)/shard_map/while/body/eval_jaxpr/ppermute | solution.py:15
Sparse Core Ops, SparseCore 0:
  9.5 51.7 all-gather.6
  62.9 32.9 all-gather.4
  98.0 72.7 all-gather.8
  172.8 80.7 all-gather.10
  260.2 45.0 reduce-scatter.1
where the time goes:
time: 312 us
  waiting for transfers between devices  249 us (80%)
  matrix products  24.9 us (8%)
  between operations  13.3 us (4%)
  starting transfers between devices  11.4 us (4%)
  other arithmetic  11 us (4%)
    all_gather x1, waiting for transfers between devices, on_device(): lax.all_gather(w_query, 'blk', axis=0, tiled=True)  69.1 us
    all_gather x1, waiting for transfers between devices, on_device(): lax.all_gather(key_value_weight, 'blk', axis=0, tiled=True)  46.9 us
    reduce_scatter x1, waiting for transfers between devices, on_device(): lax.psum_scatter(jnp.dot(mixed, head_rows, preferred_element_type=jnp.flo...  45.2 us
    all_gather x1, waiting for transfers between devices, on_device(): head_rows = lax.all_gather(w_out, 'blk', axis=0, tiled=True)  41.3 us
    all_gather x1, waiting for transfers between devices, on_device(): block_input = lax.all_gather(normalized_input, 'heads', axis=0, tiled=True)  34.6 us
    ppermute x2, starting transfers between devices, shifted(): lax.ppermute(value, axis, [(source, source + steps) for source in range(f...  11.3 us
    ppermute x2, waiting for transfers between devices, shifted(): lax.ppermute(value, axis, [(source, source + steps) for source in range(f...  9.5 us
    dot_general x1, matrix products, on_device(): jnp.dot(mixed, head_rows, preferred_element_type=jnp.float32)  6.52 us
  transfers between devices with their start and end apart: 7, of which 7 were waited for; matrix products, arithmetic and copies ran while one was open for 10% of the time, Pallas kernels for 0%

commit v1 on v0

--- a/solution.py
+++ b/solution.py
@@ -120,7 +120,15 @@
     highest, totals, accum = state
     mixed = accum / totals[..., None]
     mixed = mixed.transpose(2, 0, 1, 3).reshape(block_rows, query_cols).astype(jnp.bfloat16)
-    head_rows = lax.all_gather(w_out, "blk", axis=0, tiled=True)
+    parts_n = lax.axis_size("blk")
+    prior = [(num - 1, num) for num in range(1, parts_n)] + [(parts_n - 1, 0)]
+    row_out = w_out
+    pile = [row_out]
+    for _ in range(parts_n - 1):
+        row_out = lax.ppermute(row_out, axis_name="blk", perm=prior)
+        pile += [row_out]
+    mid_arr = jnp.concatenate([*reversed(pile)], axis=0)
+    head_rows = jnp.roll(mid_arr, (lax.axis_index("blk") + 1) * row_out.shape[0], axis=0)
     return lax.psum_scatter(
         jnp.dot(mixed, head_rows, preferred_element_type=jnp.float32).astype(jnp.bfloat16),
         "heads",

time: 312 us -> 294 us (0.942)
  waiting for transfers between devices: 249 us -> 213 us
  local copies, waits for them, and re-layouts: 2.21 us -> 19.9 us
    ppermute x0 -> x7, waiting for transfers between devices: none -> 112 us  [on_device(): row_out = lax.ppermute(row_out, axis_name='blk', perm=prior)]
    all_gather x1, waiting for transfers between devices: 46.9 us -> 0.01 us  [on_device(): lax.all_gather(key_value_weight, 'blk', axis=0, tiled=True)]
    all_gather x1 -> x0, waiting for transfers between devices: 41.3 us -> none  [on_device(): head_rows = lax.all_gather(w_out, 'blk', axis=0, tiled=True)]
    all_gather x1, waiting for transfers between devices: 34.6 us -> 0.01 us  [on_device(): block_input = lax.all_gather(normalized_input, 'heads', axis=0, tiled=True)]
    all_gather x1, waiting for transfers between devices: 69.1 us -> 43.4 us  [on_device(): lax.all_gather(w_query, 'blk', axis=0, tiled=True)]
    unnamed x11 -> x32, local copies, waits for them, and re-layouts: 1.69 us -> 18.5 us
    ppermute x2, starting transfers between devices: 11.3 us -> 6.88 us  [shifted(): lax.ppermute(value, axis, [(source, source + steps) for source in range(f...]
    reduce_scatter x1, waiting for transfers between devices: 45.2 us -> 48.8 us  [on_device(): lax.psum_scatter(jnp.dot(mixed, head_rows, preferred_element_type=jnp.flo...]
  transfers between devices with their start and end apart: 7 -> 13, of which waited for: 7 -> 11; matrix products, arithmetic and copies ran while one was open for 10% -> 10% of each run, Pallas kernels for 0% -> 0%
where the time goes in v1:
time: 294 us; the launch traced here: 293 us
  waiting for transfers between devices  213 us (72%)
  matrix products  24.9 us (8%)
  local copies, waits for them, and re-layouts  19.9 us (7%)
  between operations  13.4 us (5%)
  other arithmetic  11.9 us (4%)
  starting transfers between devices  10 us (3%)
    ppermute x7, waiting for transfers between devices, on_device(): row_out = lax.ppermute(row_out, axis_name='blk', perm=prior)  112 us
    reduce_scatter x1, waiting for transfers between devices, on_device(): lax.psum_scatter(jnp.dot(mixed, head_rows, preferred_element_type=jnp.flo...  48.8 us
    all_gather x1, waiting for transfers between devices, on_device(): lax.all_gather(w_query, 'blk', axis=0, tiled=True)  43.4 us
    unnamed x32, local copies, waits for them, and re-layouts  18.5 us
    ppermute x2, waiting for transfers between devices, shifted(): lax.ppermute(value, axis, [(source, source + steps) for source in range(f...  7.25 us
    ppermute x2, starting transfers between devices, shifted(): lax.ppermute(value, axis, [(source, source + steps) for source in range(f...  6.88 us
    dot_general x1, matrix products, on_device(): jnp.dot(mixed, head_rows, preferred_element_type=jnp.float32)  6.54 us
  transfers between devices with their start and end apart: 13, of which 11 were waited for; matrix products, arithmetic and copies ran while one was open for 10% of the time, Pallas kernels for 0%

profile of v1, /device:TPU:0, one launch (start us, length us, event | category | flops | bytes accessed | tf_op | source)
XLA Modules:
  0.0 293.2 jit_solution(9226203539502205790)
XLA Ops:
  7.3 1.5 fusion.25
  8.8 2.5 fusion.26
  11.4 3.0 %collective-permute-start.1 = (bf16[64,4096]{1,0:T(8,128)(2,1)S(1)}, bf16[64,4096]{1,0:T(8,128)(2,1)S(1)}, u32[]{:S(2)}, u32[]{:S(2)}) collective-permute-start(bf16[64,4096]{1,0:T(8,128)(2,1)S(1)} %copy-done), channel_id=1, source_target_pairs={{0,1},{1,2},{2,3},{3,4},{4,5},{5,6},{6,7},{7,0},{8,9},{9,10},{10,1... | collective-permute-start | bytes 1572872 | tf_op jit(solution)/shard_map/ppermute | solution.py:128
  14.4 19.4 %collective-permute-done.1 = bf16[64,4096]{1,0:T(8,128)(2,1)S(1)} collective-permute-done((bf16[64,4096]{1,0:T(8,128)(2,1)S(1)}, bf16[64,4096]{1,0:T(8,128)(2,1)S(1)}, u32[]{:S(2)}, u32[]{:S(2)}) %collective-permute-start.1) | collective-permute-done | bytes 524320 | tf_op jit(solution)/shard_map/ppermute | solution.py:128
  33.8 15.3 %collective-permute-done.2 = bf16[64,4096]{1,0:T(8,128)(2,1)S(1)} collective-permute-done((bf16[64,4096]{1,0:T(8,128)(2,1)S(1)}, bf16[64,4096]{1,0:T(8,128)(2,1)S(1)}, u32[]{:S(2)}, u32[]{:S(2)}) %collective-permute-start.2) | collective-permute-done | bytes 524320 | tf_op jit(solution)/shard_map/ppermute | solution.py:128
  49.0 25.4 %collective-permute-done.3 = bf16[64,4096]{1,0:T(8,128)(2,1)S(1)} collective-permute-done((bf16[64,4096]{1,0:T(8,128)(2,1)S(1)}, bf16[64,4096]{1,0:T(8,128)(2,1)S(1)}, u32[]{:S(2)}, u32[]{:S(2)}) %collective-permute-start.3) | collective-permute-done | bytes 524320 | tf_op jit(solution)/shard_map/ppermute | solution.py:128
  74.4 17.2 %collective-permute-done.4 = bf16[64,4096]{1,0:T(8,128)(2,1)S(1)} collective-permute-done((bf16[64,4096]{1,0:T(8,128)(2,1)S(1)}, bf16[64,4096]{1,0:T(8,128)(2,1)S(1)}, u32[]{:S(2)}, u32[]{:S(2)}) %collective-permute-start.4) | collective-permute-done | bytes 524320 | tf_op jit(solution)/shard_map/ppermute | solution.py:128
  91.9 12.9 %collective-permute-done.5 = bf16[64,4096]{1,0:T(8,128)(2,1)S(1)} collective-permute-done((bf16[64,4096]{1,0:T(8,128)(2,1)S(1)}, bf16[64,4096]{1,0:T(8,128)(2,1)S(1)}, u32[]{:S(2)}, u32[]{:S(2)}) %collective-permute-start.5) | collective-permute-done | bytes 524320 | tf_op jit(solution)/shard_map/ppermute | solution.py:128
  105.0 12.4 %collective-permute-done.6 = bf16[64,4096]{1,0:T(8,128)(2,1)} collective-permute-done((bf16[64,4096]{1,0:T(8,128)(2,1)S(1)}, bf16[64,4096]{1,0:T(8,128)(2,1)}, u32[]{:S(2)}, u32[]{:S(2)}) %collective-permute-start.6) | collective-permute-done | bytes 524320 | tf_op jit(solution)/shard_map/ppermute | solution.py:128
  117.7 1.8 multiply_cosine_fusion
  119.5 10.0 %collective-permute-done.7 = bf16[64,4096]{1,0:T(8,128)(2,1)} collective-permute-done((bf16[64,4096]{1,0:T(8,128)(2,1)}, bf16[64,4096]{1,0:T(8,128)(2,1)}, u32[]{:S(2)}, u32[]{:S(2)}) %collective-permute-start.7) | collective-permute-done | bytes 524320 | tf_op jit(solution)/shard_map/ppermute | solution.py:128
  129.5 1.9 constant_dynamic-update-slice_fusion.15
  131.4 1.9 constant_dynamic-update-slice_fusion.14
  138.3 1.9 constant_dynamic-update-slice_fusion.7
  140.2 1.9 constant_dynamic-update-slice_fusion.6
  147.2 4.2 %fusion.28 = f32[512,256]{0,1:T(8,128)S(1)} fusion(bf16[512,4096]{1,0:T(8,128)(2,1)} %all-gather.4.cloned.1.call-done, bf16[512,8,2,128]{3,2,1,0:T(2,128)(2,1)} %bitcast.160), kind=kOutput, calls=%fused_computation.39 | convolution fusion | flops 1073741824 | bytes 6815744 | tf_op jit(solution)/shard_map/dot_general | solution.py:56
  152.8 43.4 %all-gather.8.cloned.1.call-done = bf16[4096,512]{1,0:T(8,128)(2,1)} async-done(((bf16[512,512]{1,0:T(8,128)(2,1)}), bf16[4096,512]{1,0:T(8,128)(2,1)}) %all-gather.8.cloned.1.call-update) | async-done | bytes 4194320 | tf_op jit(solution)/shard_map/all_gather | solution.py:51
  196.3 5.8 %fusion.66 = f32[512,512]{0,1:T(8,128)S(1)} fusion(bf16[512,4096]{1,0:T(8,128)(2,1)} %all-gather.4.cloned.1.call-done, bf16[4096,512]{1,0:T(8,128)(2,1)} %all-gather.8.cloned.1.call-done), kind=kOutput, calls=%fused_computation.110 | convolution fusion | flops 2147483648 | bytes 9437184 | tf_op jit(solution)/shard_map/dot_general | solution.py:55
  203.5 1.2 fusion.22
  204.7 1.1 fusion.24
  205.8 1.6 fusion.37
  207.7 23.1 %while.22 = (s32[]{:T(128)}, bf16[512,2,1,128]{3,0,2,1:T(8,128)(2,1)S(1)}, f32[1,4,512]{2,1,0:T(4,128)S(1)}, f32[1,4,512]{2,1,0:T(4,128)S(1)}, f32[1,4,512,128]{...) while((s32[]{:T(128)}, ...), condition=%wide.region_10.11_spmd.clone, body=%wide.region_6.10_spmd.clone.sunk | while | flops 552107520 | bytes 18236672 | solution.py:119
  207.9 2.5 collective-permute-start
  210.8 3.9 %collective-permute-done = bf16[512,2,1,128]{3,0,2,1:T(8,128)(2,1)S(1)} collective-permute-done((bf16[512,2,1,128]{3,0,2,1:T(8,128)(2,1)S(1)}, bf16[512,2,1,128]{3,0,2,1:T(8,128)(2,1)S(1)}, u32[]{:S(2)}, u32[]{:S(2)}) %collective-permute-start) | collective-permute-done | bytes 262176 | tf_op jit(solution)/shard_map/while/body/eval_jaxpr/ppermute | solution.py:15
  215.6 1.0 fusion.79
  216.7 1.9 fusion.80
  218.6 4.4 %collective-permute-start = (bf16[512,2,1,128]{3,0,2,1:T(8,128)(2,1)S(1)}, bf16[512,2,1,128]{3,0,2,1:T(8,128)(2,1)S(1)}, u32[]{:S(2)}, u32[]{:S(2)}) collective-permute-start(bf16[512,2,1,128]{3,0,2,1:T(8,128)(2,1)S(1)} %get-tuple-element.431), channel_id=1, source_target_pairs={{0,1},{1,2},{2,3},{3,4},{4,5},{5,6},{6,7},{8,9},{9,10},{10,11},{11... | collective-permute-start | bytes 786440 | tf_op jit(solution)/shard_map/while/body/eval_jaxpr/ppermute | solution.py:15
  223.5 3.4 %collective-permute-done = bf16[512,2,1,128]{3,0,2,1:T(8,128)(2,1)S(1)} collective-permute-done((bf16[512,2,1,128]{3,0,2,1:T(8,128)(2,1)S(1)}, bf16[512,2,1,128]{3,0,2,1:T(8,128)(2,1)S(1)}, u32[]{:S(2)}, u32[]{:S(2)}) %collective-permute-start) | collective-permute-done | bytes 262176 | tf_op jit(solution)/shard_map/while/body/eval_jaxpr/ppermute | solution.py:15
  227.8 1.0 fusion.79
  228.9 1.9 fusion.80
  231.3 6.5 %convolution_convert_fusion = bf16[512,4096]{1,0:T(8,128)(2,1)} fusion(bf16[512,512]{0,1:T(8,128)(2,1)S(1)} %bitcast.155, bf16[1024,4096]{1,0:T(8,128)(2,1)} %constant_dynamic-update-slice_fusion, s32[]{:T(128)S(6)} %select_n.46), kind=kOutput, calls=%fused_computation.27 | convolution fusion | flops 2149580800 | bytes 8912900 | tf_op jit(solution)/shard_map/dot_general | solution.py:133
  237.9 48.8 %reduce-scatter.2.cloned.1.call-done = bf16[128,4096]{1,0:T(8,128)(2,1)} async-done(((bf16[512,4096]{1,0:T(8,128)(2,1)}), bf16[128,4096]{1,0:T(8,128)(2,1)}) %reduce-scatter.2.cloned.1.call-update) | async-done | bytes 1048592 | tf_op jit(solution)/shard_map/reduce_scatter | solution.py:132
  (82 shorter events, 17.9 us)
Async XLA Ops:
  6.5 4.8 %copy-start = (bf16[64,4096]{1,0:T(8,128)(2,1)S(1)}, bf16[64,4096]{1,0:T(8,128)(2,1)}, u32[]{:S(2)}) copy-start(bf16[64,4096]{1,0:T(8,128)(2,1)} %param.10) | copy-start | bytes 1572868
  6.5 85.2 %copy-start.6 = (s32[16]{0:T(128)S(1)}, s32[16]{0:T(128)}, u32[]{:S(2)}) copy-start(s32[16]{0:T(128)} %param.11) | copy-start | bytes 196
  6.5 140.6 %all-gather.6.cloned.1.call-start = ((), (), s32[]{:S(2)}) async-start(), calls=%async_computation.2 | async-start | bytes 2359296 | tf_op jit(solution)/shard_map/all_gather | solution.py:52
  7.3 139.9 %all-gather.4.cloned.1.call-start = ((), (), s32[]{:S(2)}) async-start(), calls=%async_computation.1 | async-start | bytes 5242880 | tf_op jit(solution)/shard_map/all_gather | solution.py:46
  11.3 185.0 %all-gather.8.cloned.1.call-start = ((), (), s32[]{:S(2)}) async-start(), calls=%async_computation.3 | async-start | bytes 4718592 | tf_op jit(solution)/shard_map/all_gather | solution.py:51
  11.4 22.4 %collective-permute-start.1 = (bf16[64,4096]{1,0:T(8,128)(2,1)S(1)}, bf16[64,4096]{1,0:T(8,128)(2,1)S(1)}, u32[]{:S(2)}, u32[]{:S(2)}) collective-permute-start(bf16[64,4096]{1,0:T(8,128)(2,1)S(1)} %copy-done), channel_id=1, source_target_pairs={{0,1},{1,2},{2,3},{3,4},{4,5},{5,6},{6,7},{7,0},{8,9},{9,10},{10,1... | collective-permute-start | bytes 1572872 | tf_op jit(solution)/shard_map/ppermute | solution.py:128
  33.8 15.3 %collective-permute-start.2 = (bf16[64,4096]{1,0:T(8,128)(2,1)S(1)}, bf16[64,4096]{1,0:T(8,128)(2,1)S(1)}, u32[]{:S(2)}, u32[]{:S(2)}) collective-permute-start(bf16[64,4096]{1,0:T(8,128)(2,1)S(1)} %collective-permute-done.1), channel_id=1, source_target_pairs={{0,1},{1,2},{2,3},{3,4},{4,5},{5,6},{6,7},{7,0},{8,9},{9,10},{10,1... | collective-permute-start | bytes 1572872 | tf_op jit(solution)/shard_map/ppermute | solution.py:128
  49.0 25.4 %collective-permute-start.3 = (bf16[64,4096]{1,0:T(8,128)(2,1)S(1)}, bf16[64,4096]{1,0:T(8,128)(2,1)S(1)}, u32[]{:S(2)}, u32[]{:S(2)}) collective-permute-start(bf16[64,4096]{1,0:T(8,128)(2,1)S(1)} %collective-permute-done.2), channel_id=1, source_target_pairs={{0,1},{1,2},{2,3},{3,4},{4,5},{5,6},{6,7},{7,0},{8,9},{9,10},{10,1... | collective-permute-start | bytes 1572872 | tf_op jit(solution)/shard_map/ppermute | solution.py:128
  74.4 17.2 %collective-permute-start.4 = (bf16[64,4096]{1,0:T(8,128)(2,1)S(1)}, bf16[64,4096]{1,0:T(8,128)(2,1)S(1)}, u32[]{:S(2)}, u32[]{:S(2)}) collective-permute-start(bf16[64,4096]{1,0:T(8,128)(2,1)S(1)} %collective-permute-done.3), channel_id=1, source_target_pairs={{0,1},{1,2},{2,3},{3,4},{4,5},{5,6},{6,7},{7,0},{8,9},{9,10},{10,1... | collective-permute-start | bytes 1572872 | tf_op jit(solution)/shard_map/ppermute | solution.py:128
  91.6 13.2 %collective-permute-start.5 = (bf16[64,4096]{1,0:T(8,128)(2,1)S(1)}, bf16[64,4096]{1,0:T(8,128)(2,1)S(1)}, u32[]{:S(2)}, u32[]{:S(2)}) collective-permute-start(bf16[64,4096]{1,0:T(8,128)(2,1)S(1)} %collective-permute-done.4), channel_id=1, source_target_pairs={{0,1},{1,2},{2,3},{3,4},{4,5},{5,6},{6,7},{7,0},{8,9},{9,10},{10,1... | collective-permute-start | bytes 1572872 | tf_op jit(solution)/shard_map/ppermute | solution.py:128
  91.6 195.0 %reduce-scatter.2.cloned.1.call-start = ((), (), s32[]{:S(2)}) async-start(), calls=%async_computation.4 | async-start | bytes 5242880 | tf_op jit(solution)/shard_map/reduce_scatter | solution.py:132
  104.8 12.5 %collective-permute-start.6 = (bf16[64,4096]{1,0:T(8,128)(2,1)S(1)}, bf16[64,4096]{1,0:T(8,128)(2,1)}, u32[]{:S(2)}, u32[]{:S(2)}) collective-permute-start(bf16[64,4096]{1,0:T(8,128)(2,1)S(1)} %collective-permute-done.5), channel_id=1, source_target_pairs={{0,1},{1,2},{2,3},{3,4},{4,5},{5,6},{6,7},{7,0},{8,9},{9,10},{10,1... | collective-permute-start | bytes 1572872 | tf_op jit(solution)/shard_map/ppermute | solution.py:128
  117.3 12.2 %collective-permute-start.7 = (bf16[64,4096]{1,0:T(8,128)(2,1)}, bf16[64,4096]{1,0:T(8,128)(2,1)}, u32[]{:S(2)}, u32[]{:S(2)}) collective-permute-start(bf16[64,4096]{1,0:T(8,128)(2,1)} %collective-permute-done.6), channel_id=1, source_target_pairs={{0,1},{1,2},{2,3},{3,4},{4,5},{5,6},{6,7},{7,0},{8,9},{9,10},{10,1... | collective-permute-start | bytes 1572872 | tf_op jit(solution)/shard_map/ppermute | solution.py:128
  151.3 44.9 %copy-start.3 = (f32[512,256]{0,1:T(8,128)}, f32[512,256]{0,1:T(8,128)S(1)}, u32[]{:S(2)}) copy-start(f32[512,256]{0,1:T(8,128)S(1)} %fusion.28) | copy-start | bytes 1572868
  202.1 1.0 copy-start.1
  202.1 1.0 copy-start.2
  203.5 2.3 copy-start.4
  205.8 1.9 copy-start.5
  207.9 6.8 %collective-permute-start = (bf16[512,2,1,128]{3,0,2,1:T(8,128)(2,1)S(1)}, bf16[512,2,1,128]{3,0,2,1:T(8,128)(2,1)S(1)}, u32[]{:S(2)}, u32[]{:S(2)}) collective-permute-start(bf16[512,2,1,128]{3,0,2,1:T(8,128)(2,1)S(1)} %get-tuple-element.431), channel_id=1, source_target_pairs={{0,1},{1,2},{2,3},{3,4},{4,5},{5,6},{6,7},{8,9},{9,10},{10,11},{11... | collective-permute-start | bytes 786440 | tf_op jit(solution)/shard_map/while/body/eval_jaxpr/ppermute | solution.py:15
  218.6 8.3 %collective-permute-start = (bf16[512,2,1,128]{3,0,2,1:T(8,128)(2,1)S(1)}, bf16[512,2,1,128]{3,0,2,1:T(8,128)(2,1)S(1)}, u32[]{:S(2)}, u32[]{:S(2)}) collective-permute-start(bf16[512,2,1,128]{3,0,2,1:T(8,128)(2,1)S(1)} %get-tuple-element.431), channel_id=1, source_target_pairs={{0,1},{1,2},{2,3},{3,4},{4,5},{5,6},{6,7},{8,9},{9,10},{10,11},{11... | collective-permute-start | bytes 786440 | tf_op jit(solution)/shard_map/while/body/eval_jaxpr/ppermute | solution.py:15
Sparse Core Ops, SparseCore 0:
  9.5 73.8 all-gather.5
  84.9 36.3 all-gather.3
  123.4 72.8 all-gather.7
  238.0 48.6 reduce-scatter.1
